TPU v7x, 32 devices: a whole 2x2x4 slice. The times are simulated.
32 devices in a mesh: dp: 8 (over y, x, core), mp: 4 (over z).
Axes of the slice: x: 2, y: 2, z: 4, core: 2. Of those that a mesh axis runs over, the one named last changes fastest.
Arguments:
- tokens: bfloat16 [12288, 4096], P('dp'), may hold values from -40 to 40
- norm_gain: bfloat16 [4096], replicated, may hold values from 0.099609375 to 1.8984375
- w_query: bfloat16 [4096, 2048], P(None, 'mp'), may hold values from -1 to 1
- w_key: bfloat16 [4096, 512], P(None, 'mp'), may hold values from -4 to 4
- w_value: bfloat16 [4096, 512], P(None, 'mp'), may hold values from -0.09375 to 0.09375
- w_out: bfloat16 [2048, 4096], P('mp'), may hold values from -0.125 to 0.125
- seq_starts: int32 [64], P('dp'), may hold values from 0 to 1408, as said below
- seq_lengths: int32 [64], P('dp'), may hold values from 128 to 640
- episode_ids: int32 [64], replicated, may hold values from 0 to 0, as said below
- class_ids: int32 [64], replicated, may hold values from 0 to 31
- query_flags: int32 [64], replicated, may hold values from 0 to 1
Outputs:
- log_probs: float32 [64, 32], P('dp')
- prototypes: float32 [32, 4096], P(None, 'mp')
Inputs may be any that keep to these rules, and one draw needn't show every extreme that they name: `seq_starts`: slot s lies in the buffer of dp index s // 8; the slots of one buffer are disjoint and in increasing order of start; start plus length is at most 1536, and in every draw the last slot of some buffer ends at row 1536. `episode_ids`: every class of every episode has at least one support sequence.
All inputs are finite; a program needn't handle non-finite values.
Results may differ from a plain program's by a relative error of at most 0.004.
Values sent between devices are 32-bit elements; how exact they have to be, the bound alone decides.
No kernel may reach another device: no remote copies, remote signals or barrier semaphores. Data moves between devices by JAX's collectives and lax.ppermute only.
A program may use at most 128 MiB of HBM per device.

v0:
```python
import math
import jax
import jax.numpy as jnp
from jax import lax
from jax.sharding import PartitionSpec as P

HEAD_DIM = 128
WAYS = 32
ROPE_BASE = 500000.0
NEG_FILL = -1e30


def rotate(vectors, positions):
    half_dim = vectors.shape[-1] // 2
    frequency = jnp.power(
        ROPE_BASE, -(jnp.arange(half_dim, dtype=jnp.float32) * 2.0 / vectors.shape[-1])
    )
    angles = positions.astype(jnp.float32)[:, None] * frequency[None, :]
    cosine = jnp.cos(angles)[:, None, :]
    sine_part = jnp.sin(angles)[:, None, :]
    leading = vectors[..., :half_dim]
    trailing = vectors[..., half_dim:]
    return jnp.concatenate(
        [leading * cosine - trailing * sine_part, trailing * cosine + leading * sine_part], axis=-1
    )


def layout_of(starts, lengths, buffer_len):
    token_index = jnp.arange(buffer_len, dtype=jnp.int32)
    inside = (token_index[:, None] >= starts[None, :]) & (
        token_index[:, None] < (starts + lengths)[None, :]
    )
    slot_number = jnp.arange(starts.shape[0], dtype=jnp.int32)
    segment = jnp.sum(jnp.where(inside, slot_number[None, :] + 1, 0), axis=1) - 1
    position = jnp.sum(jnp.where(inside, token_index[:, None] - starts[None, :], 0), axis=1)
    return (segment, position, inside)


def allowed_mask(segment, row_start, row_count, col_count):
    rows_index = row_start + jnp.arange(row_count, dtype=jnp.int32)
    cols_index = jnp.arange(col_count, dtype=jnp.int32)
    seg_rows = segment[row_start : row_start + row_count]
    seg_cols = segment[:col_count]
    same = (
        (seg_rows[:, None] == seg_cols[None, :])
        & (seg_rows[:, None] >= 0)
        & (cols_index[None, :] < rows_index[:, None])
    )
    return (rows_index[:, None] == cols_index[None, :]) | same


def softmax_rows(scores, permitted):
    masked_scores = jnp.where(permitted[None, None], scores, NEG_FILL)
    row_peak = jnp.max(masked_scores, axis=-1, keepdims=True)
    exponent = jnp.exp(masked_scores - row_peak)
    totals = jnp.sum(exponent, axis=-1, keepdims=True)
    return (exponent / totals).astype(jnp.bfloat16)


def pick_block(length_rows):
    for candidate in (512, 384, 256, 128):
        return candidate
    return length_rows


def per_device(
    tokens,
    norm_gain,
    w_query,
    w_key,
    w_value,
    w_out,
    seq_starts,
    seq_lengths,
    episode_ids,
    class_ids,
    query_flags,
):
    buffer_len = tokens.shape[0]
    model_width = tokens.shape[1]
    seq_count = seq_starts.shape[0]
    head_dim = HEAD_DIM
    heads_local = w_query.shape[1] // head_dim
    kv_local = w_key.shape[1] // head_dim
    group_size = heads_local // kv_local
    inv_root = 1.0 / math.sqrt(head_dim)
    highest = lax.Precision.HIGHEST
    segment, position, inside = layout_of(seq_starts, seq_lengths, buffer_len)
    widened = tokens.astype(jnp.float32)
    normed = (
        widened
        * lax.rsqrt(jnp.mean(widened * widened, axis=-1, keepdims=True) + 1e-05)
        * norm_gain.astype(jnp.float32)
    ).astype(jnp.bfloat16)
    queries = rotate(
        jnp.dot(normed, w_query, preferred_element_type=jnp.float32).reshape(
            buffer_len, heads_local, head_dim
        ),
        position,
    ).astype(jnp.bfloat16)
    queries = queries.reshape(buffer_len, kv_local, group_size, head_dim)
    keys_rot = rotate(
        jnp.dot(normed, w_key, preferred_element_type=jnp.float32).reshape(
            buffer_len, kv_local, head_dim
        ),
        position,
    ).astype(jnp.bfloat16)
    values_all = (
        jnp.dot(normed, w_value, preferred_element_type=jnp.float32)
        .astype(jnp.bfloat16)
        .reshape(buffer_len, kv_local, head_dim)
    )
    block_rows = pick_block(buffer_len)
    block_count = buffer_len // block_rows
    mixed_blocks = []
    for query_block in range(block_count):
        row_start = query_block * block_rows
        key_end = row_start + block_rows
        block_queries = queries[row_start:key_end]
        permitted = allowed_mask(segment, row_start, block_rows, key_end)
        scores = (
            jnp.einsum(
                "qngd,knd->ngqk",
                block_queries,
                keys_rot[:key_end],
                preferred_element_type=jnp.float32,
            )
            * inv_root
        )
        attention_probs = softmax_rows(scores, permitted)
        mixed_out = jnp.einsum(
            "ngqk,knd->qngd",
            attention_probs,
            values_all[:key_end],
            preferred_element_type=jnp.float32,
        )
        mixed_blocks.append(
            mixed_out.astype(jnp.bfloat16).reshape(block_rows, heads_local * head_dim)
        )
    attended = jnp.concatenate(mixed_blocks, axis=0)
    member = inside.T.astype(jnp.bfloat16)
    attended_sums = jnp.dot(member, attended, preferred_element_type=jnp.float32)
    token_sums = jnp.dot(member, tokens, preferred_element_type=jnp.float32)
    high_part = attended_sums.astype(jnp.bfloat16)
    low_part = (attended_sums - high_part.astype(jnp.float32)).astype(jnp.bfloat16)
    head_part = jnp.dot(high_part, w_out, preferred_element_type=jnp.float32) + jnp.dot(
        low_part, w_out, preferred_element_type=jnp.float32
    )
    token_counts = seq_lengths.astype(jnp.float32)[:, None]
    mp_size = lax.axis_size("mp")
    mp_rank = lax.axis_index("mp")
    share_cols = model_width // mp_size
    pooled = (token_sums + lax.psum(head_part, "mp")) / token_counts
    embedded = pooled * lax.rsqrt(jnp.mean(pooled * pooled, axis=-1, keepdims=True) + 1e-06)
    seq_total = episode_ids.shape[0]
    episodes = max(1, seq_total // (2 * WAYS))
    classes = episodes * WAYS
    global_class = episode_ids * WAYS + class_ids
    is_support = query_flags == 0
    class_range = jnp.arange(classes, dtype=jnp.int32)
    select_all = ((global_class[None, :] == class_range[:, None]) & is_support[None, :]).astype(
        jnp.float32
    )
    dp_first = lax.axis_index("dp") * seq_count
    class_sums = jnp.dot(
        select_all, lax.all_gather(embedded, "dp", axis=0, tiled=True), precision=highest
    )
    proto_scale = jnp.mean(class_sums * class_sums, axis=-1)
    prototypes = class_sums * lax.rsqrt(proto_scale + 1e-06)[:, None]
    difference = embedded[:, None, :] - prototypes[None, :, :]
    distance = jnp.sum(difference * difference, axis=-1)
    proto_out = lax.dynamic_slice_in_dim(prototypes, mp_rank * share_cols, share_cols, 1)
    own_episode = lax.dynamic_slice_in_dim(episode_ids, dp_first, seq_count, 0)
    own_query = lax.dynamic_slice_in_dim(query_flags, dp_first, seq_count, 0)
    episode_range = jnp.arange(episodes, dtype=jnp.int32)
    picked = jnp.sum(
        jnp.where(
            own_episode[:, None, None] == episode_range[None, :, None],
            distance.reshape(seq_count, episodes, WAYS),
            0.0,
        ),
        axis=1,
    )
    logits = -picked / math.sqrt(model_width)
    row_peak = jnp.max(logits, axis=-1, keepdims=True)
    shifted = logits - row_peak
    log_probs = shifted - jnp.log(jnp.sum(jnp.exp(shifted), axis=-1, keepdims=True))
    log_probs = jnp.where(own_query[:, None] == 1, log_probs, 0.0)
    return (log_probs, proto_out)


def solution(mesh):
    placed = (
        P("dp", None),
        P(),
        P(None, "mp"),
        P(None, "mp"),
        P(None, "mp"),
        P("mp", None),
        P("dp"),
        P("dp"),
        P(),
        P(),
        P(),
    )
    return jax.shard_map(
        per_device,
        mesh=mesh,
        in_specs=placed,
        out_specs=(P("dp", None), P(None, "mp")),
        check_vma=False,
    )
```

profile of v0, /device:TPU:0, one launch (start us, length us, event | category | flops | bytes accessed | tf_op | source)
XLA Modules:
  0.0 166.5 jit_solution(195916968314349228)
XLA Ops:
  8.9 7.1 %fusion = f32[1536]{0:T(1024)S(1)} fusion(bf16[1536,4096]{1,0:T(8,128)(2,1)} %param.11), kind=kLoop, calls=%fused_computation.2 | loop fusion | flops 18872832 | bytes 12589056 | tf_op jit(solution)/shard_map/reduce_sum | solution.py:92
  16.0 7.9 %fusion.2 = bf16[1536,4096]{1,0:T(8,128)(2,1)S(1)} fusion(bf16[1536,4096]{1,0:T(8,128)(2,1)} %param.11, f32[4096]{0:T(1024)S(1)} %convert_element_type.82, f32[1536]{0:T(1024)S(1)} %add_rsqrt_fusion), kind=kLoop, calls=%fused_computation.4 | loop fusion | flops 25165824 | bytes 25188352 | tf_op jit(solution)/shard_map/convert_element_type | solution.py:94
  23.9 3.4 %convolution_convert_fusion = bf16[1536,128]{1,0:T(8,128)(2,1)S(1)} fusion(bf16[1536,4096]{1,0:T(8,128)(2,1)S(1)} %fusion.2, bf16[4096,128]{1,0:T(8,128)(2,1)S(1)} %copy-done), kind=kOutput, calls=%fused_computation.35 | convolution fusion | flops 1610809344 | bytes 14024704 | tf_op jit(solution)/shard_map/dot_general | solution.py:109
  27.3 5.5 %convolution_bitcast_fusion = f32[1536,1,128]{0,2,1:T(8,128)S(1)} fusion(bf16[1536,4096]{1,0:T(8,128)(2,1)S(1)} %fusion.2, bf16[4096,128]{1,0:T(8,128)(2,1)} %param.14), kind=kOutput, calls=%fused_computation.34 | convolution fusion | flops 1610612736 | bytes 14417920 | tf_op jit(solution)/shard_map/dot_general | solution.py:103
  32.9 9.7 %fusion.87 = f32[1536,512]{0,1:T(8,128)} fusion(bf16[1536,4096]{1,0:T(8,128)(2,1)S(1)} %fusion.2, bf16[4096,512]{1,0:T(8,128)(2,1)} %param.13), kind=kOutput, calls=%fused_computation.142 | convolution fusion | flops 6442450944 | bytes 19922944 | tf_op jit(solution)/shard_map/dot_general | solution.py:96
  42.5 4.3 %multiply_cosine_fusion = (f32[1536,64]{1,0:T(8,128)}, f32[1536,64]{1,0:T(8,128)}) fusion(f32[64]{0:T(128)S(1)} %negate_power_fusion, f32[1536]{0:T(1024)S(1)} %convert_element_type.85), kind=kLoop, calls=%fused_computation.57 | loop fusion | flops 98304 | bytes 792832 | tf_op jit(solution)/shard_map/cos | solution.py:19
  46.8 1.6 fusion.51
  48.4 3.3 %fusion.84 = (f32[1536,4,64]{0,2,1:T(8,128)}, f32[1536,4,64]{0,2,1:T(8,128)S(1)}) fusion(f32[1536,4,128]{0,2,1:T(8,128)} %bitcast.120), kind=kLoop, calls=%fused_computation.139 | loop fusion | bytes 6291456 | tf_op jit(solution)/shard_map/slice | solution.py:22
  51.7 3.3 %copy.51 = f32[1536,4,64]{2,0,1:T(8,128)} copy(f32[1536,4,64]{0,2,1:T(8,128)} %get-tuple-element.6) | data formatting | bytes 3145728
  55.0 2.3 %copy.50 = f32[1536,4,64]{2,0,1:T(8,128)} copy(f32[1536,4,64]{0,2,1:T(8,128)S(1)} %get-tuple-element.7) | data formatting | bytes 3145728
  58.4 4.0 %subtract_convert_fusion = (bf16[1536,4,64]{2,0,1:T(8,128)(2,1)S(1)}, bf16[1536,4,64]{2,0,1:T(8,128)(2,1)S(1)}) fusion(f32[1536,4,64]{2,0,1:T(8,128)} %copy.51, f32[1536,4,64]{2,0,1:T(8,128)} %copy.50, f32[1536,64]{1,0:T(8,128)} %get-tuple-element.11, f32[1536,64]{1,0:T(8,128)} %get-tuple-element.10), kind=kLoop, calls=%fused_computation.31 | loop fusion | flops 3145728 | bytes 5505024 | tf_op jit(solution)/shard_map/convert.4
  63.6 2.0 %fusion.6 = (f32[4,512]{1,0:T(4,128)S(1)}, f32[1024,512,4]{1,0,2:T(8,128)S(1)}) fusion(pred[512,1024]{0,1:T(8,128)(4,1)S(1)} %fusion.18, bf16[1536,4,64]{2,0,1:T(8,128)(2,1)S(1)} %get-tuple-element.4, bf16[1536,4,64]{2,0,1:T(8,128)(2,1)S(1)} %get-tuple-element.5, bf16[1536,1,64]{0,2,1:T(8,128)(2,1)S(1)} %get-tuple-element.9, ...), kind=kOutput, calls=%fused_computation.14 | convolution fusion | flops 544733184 | bytes 10887168 | tf_op jit(solution)/shard_map/qngd,knd->ngqk/dot_general | solution.py:122
  66.6 1.5 fusion.30
  68.0 1.9 %fusion.5 = f32[4,512]{1,0:T(4,128)S(1)} fusion(f32[1024,512,4]{1,0,2:T(8,128)S(1)} %get-tuple-element.23, f32[4,512]{1,0:T(4,128)S(1)} %get-tuple-element.22, pred[512,1024]{0,1:T(8,128)(4,1)S(1)} %fusion.18), kind=kLoop, calls=%fused_computation.13 | loop fusion | flops 8386560 | bytes 8929280 | tf_op jit(solution)/shard_map/reduce_sum | solution.py:56
  69.9 2.7 %fusion.27 = bf16[128,4,512]{2,0,1:T(8,128)(2,1)S(1)} fusion(f32[4,512]{1,0:T(4,128)S(1)} %fusion.5, f32[4,512]{1,0:T(4,128)S(1)} %get-tuple-element.22, f32[1024,512,4]{1,0,2:T(8,128)S(1)} %get-tuple-element.23, pred[512,1024]{0,1:T(8,128)(4,1)S(1)} %fusion.18, bf16[1536,128]{1,0:T(8,128)(2,1)S(1)} %convolution_convert_fusion), kind=kOutput, calls=%fused_computation.53 | convolution fusion | flops 547618816 | bytes 9715712 | tf_op jit(solution)/shard_map/ngqk,knd->qngd/dot_general | solution.py:131
  72.6 1.7 %fusion.14 = pred[512,1536]{0,1:T(8,128)(4,1)S(1)} fusion(s32[512]{0:T(512)S(1)} %get-tuple-element.16, s32[512]{0:T(512)S(1)} %iota_add_fusion, s32[1536]{0:T(1024)S(1)} %copy-done.4, pred[512]{0:T(512)(128)(4,1)S(1)} %get-tuple-element.14), kind=kLoop, calls=%fused_computation.32 | loop fusion | flops 4718592 | bytes 797184 | tf_op jit(solution)/shard_map/or | solution.py:49
  74.4 2.8 %fusion.4 = (f32[4,512]{1,0:T(4,128)S(1)}, f32[1536,512,4]{1,0,2:T(8,128)S(1)}) fusion(pred[512,1536]{0,1:T(8,128)(4,1)S(1)} %fusion.14, bf16[1536,4,64]{2,0,1:T(8,128)(2,1)S(1)} %get-tuple-element.5, bf16[1536,4,64]{2,0,1:T(8,128)(2,1)S(1)} %get-tuple-element.4, bf16[1536,64]{0,1:T(8,128)(2,1)S(1)} %bitcast.119, bf16[1536,64]{0,1:T(8,128)(2,1)S(1)} %bitcast.118), kind=kOutput, calls=%fused_computation.9 | convolution fusion | flops 816576512 | bytes 15343616 | tf_op jit(solution)/shard_map/qngd,knd->ngqk/dot_general | solution.py:122
  77.2 2.8 %fusion.3 = f32[4,512]{1,0:T(4,128)S(1)} fusion(f32[1536,512,4]{1,0,2:T(8,128)S(1)} %get-tuple-element.21, f32[4,512]{1,0:T(4,128)S(1)} %get-tuple-element.20, pred[512,1536]{0,1:T(8,128)(4,1)S(1)} %fusion.14), kind=kLoop, calls=%fused_computation.8 | loop fusion | flops 12580864 | bytes 13385728 | tf_op jit(solution)/shard_map/reduce_sum | solution.py:56
  80.0 3.9 %fusion.33 = bf16[128,4,512]{2,0,1:T(8,128)(2,1)S(1)} fusion(f32[4,512]{1,0:T(4,128)S(1)} %fusion.3, f32[4,512]{1,0:T(4,128)S(1)} %get-tuple-element.20, f32[1536,512,4]{1,0,2:T(8,128)S(1)} %get-tuple-element.21, pred[512,1536]{0,1:T(8,128)(4,1)S(1)} %fusion.14, bf16[1536,128]{1,0:T(8,128)(2,1)S(1)} %convolution_convert_fusion), kind=kOutput, calls=%fused_computation.55 | convolution fusion | flops 821297152 | bytes 14303232 | tf_op jit(solution)/shard_map/ngqk,knd->qngd/dot_general | solution.py:131
  86.5 37.5 %all-reduce.2.cloned.1.call-done = f32[8,4096]{1,0:T(8,128)} async-done(((f32[8,4096]{1,0:T(8,128)}), f32[8,4096]{1,0:T(8,128)}) %all-reduce.2.cloned.1.call-update) | async-done | bytes 131088 | tf_op jit(solution)/shard_map/psum | solution.py:153
  124.0 6.6 %multiply_reduce_fusion.2 = (f32[8]{0:T(128)S(1)}, f32[8,4096]{1,0:T(8,128)S(1)}) fusion(f32[8]{0:T(128)S(1)} %get-tuple-element.18, f32[8,4096]{1,0:T(8,128)} %all-reduce.2.cloned.1.call-done, bf16[1536,4096]{1,0:T(8,128)(2,1)} %param.11, s32[8]{0:T(128)S(1)} %get-tuple-element.19, s32[8]{0:T(128)S(1)} %copy-done.5), kind=kOutput, calls=%fused_computation.93 | convolution fusion | flops 100831224 | bytes 12845184 | tf_op jit(solution)/shard_map/dot_general | solution.py:143
  131.4 23.1 %all-gather.2.cloned.1.call-done = f32[64,4096]{1,0:T(8,128)} async-done(((f32[8,4096]{1,0:T(8,128)}), f32[64,4096]{1,0:T(8,128)}) %all-gather.2.cloned.1.call-update) | async-done | bytes 1048592 | tf_op jit(solution)/shard_map/all_gather | solution.py:166
  154.5 1.8 %multiply_reduce_fusion.1 = (f32[32]{0:T(128)S(1)}, f32[32,4096]{1,0:T(8,128)S(1)}) fusion(f32[64,4096]{1,0:T(8,128)} %all-gather.2.cloned.1.call-done, s32[64]{0:T(128)S(1)} %multiply_add_fusion, pred[64]{0:T(512)(128)(4,1)S(1)} %broadcast_compare_fusion.3), kind=kOutput, calls=%fused_computation.75 | convolution fusion | flops 100929504 | bytes 1573312 | tf_op jit(solution)/shard_map/dot_general | solution.py:165
  156.5 1.4 multiply_reduce_fusion
  (56 shorter events, 10.1 us)
Async XLA Ops:
  7.2 16.7 %copy-start = (bf16[4096,128]{1,0:T(8,128)(2,1)S(1)}, bf16[4096,128]{1,0:T(8,128)(2,1)}, u32[]{:S(2)}) copy-start(bf16[4096,128]{1,0:T(8,128)(2,1)} %param.15) | copy-start | bytes 3145732
  7.2 116.8 %all-reduce.2.cloned.1.call-start = ((), (), s32[]{:S(2)}) async-start(), calls=%async_computation | async-start | bytes 262144 | tf_op jit(solution)/shard_map/psum | solution.py:153
  8.8 7.1 %copy-start.3 = (s32[1536]{0:T(1024)}, s32[1536]{0:T(1024)S(1)}, u32[]{:S(2)}) copy-start(s32[1536]{0:T(1024)S(1)} %broadcast_add_fusion) | copy-start | bytes 18436
  8.8 7.1 %copy-start.6 = (bf16[4096]{0:T(1024)(128)(2,1)S(1)}, bf16[4096]{0:T(1024)(128)(2,1)}, u32[]{:S(2)}) copy-start(bf16[4096]{0:T(1024)(128)(2,1)} %param.12) | copy-start | bytes 24580
  51.7 5.9 %slice-start = ((s32[1536]{0:T(1024)}), s32[1024]{0:T(1024)S(1)}, s32[]{:S(2)}) async-start(s32[1536]{0:T(1024)} %copy-done.3), calls=%async_computation.2 | async-start | bytes 8192 | tf_op jit(solution)/shard_map/slice | solution.py:43
  69.9 2.7 %copy-start.4 = (s32[1536]{0:T(1024)S(1)}, s32[1536]{0:T(1024)}, u32[]{:S(2)}) copy-start(s32[1536]{0:T(1024)} %copy-done.3) | copy-start | bytes 18436
  79.9 4.0 %copy-start.5 = (s32[8]{0:T(128)S(1)}, s32[8]{0:T(128)}, u32[]{:S(2)}) copy-start(s32[8]{0:T(128)} %param.17) | copy-start | bytes 100
  79.9 4.5 %copy-start.2 = (bf16[512,4096]{1,0:T(8,128)(2,1)S(1)}, bf16[512,4096]{1,0:T(8,128)(2,1)}, u32[]{:S(2)}) copy-start(bf16[512,4096]{1,0:T(8,128)(2,1)} %param.16) | copy-start | bytes 12582916
  86.4 68.1 %all-gather.2.cloned.1.call-start = ((), (), s32[]{:S(2)}) async-start(), calls=%async_computation.1 | async-start | bytes 1179648 | tf_op jit(solution)/shard_map/all_gather | solution.py:166
  124.0 7.4 %copy-start.7 = (s32[64]{0:T(128)S(1)}, s32[64]{0:T(128)}, u32[]{:S(2)}) copy-start(s32[64]{0:T(128)} %param.21) | copy-start | bytes 772
  124.0 7.4 %copy-start.8 = (s32[64]{0:T(128)S(1)}, s32[64]{0:T(128)}, u32[]{:S(2)}) copy-start(s32[64]{0:T(128)} %param.19) | copy-start | bytes 772
  124.0 7.5 %copy-start.9 = (s32[64]{0:T(128)S(1)}, s32[64]{0:T(128)}, u32[]{:S(2)}) copy-start(s32[64]{0:T(128)} %param.20) | copy-start | bytes 772
  124.0 35.7 %copy-start.1 = (bf16[4096,128]{1,0:T(8,128)(2,1)S(1)}, bf16[4096,128]{1,0:T(8,128)(2,1)}, u32[]{:S(2)}) copy-start(bf16[4096,128]{1,0:T(8,128)(2,1)} %param.15) | copy-start | bytes 3145732
Sparse Core Ops, SparseCore 0:
  86.6 37.3 all-reduce.1
  131.4 23.0 all-gather.1
where the time goes:
time: 167 us; the launch traced here: 166 us
  waiting for transfers between devices  60.6 us (36%)
  matrix products  43.6 us (26%)
  other arithmetic  38.3 us (23%)
  between operations  14.4 us (9%)
  local copies, waits for them, and re-layouts  9.62 us (6%)
    psum x1, waiting for transfers between devices, per_device(): pooled = (token_sums + lax.psum(head_part, 'mp')) / token_counts  37.5 us
    all_gather x1, waiting for transfers between devices, per_device(): lax.all_gather(embedded, 'dp', axis=0, tiled=True)  23.1 us
    dot_general x1, matrix products, per_device(): jnp.dot(normed, w_query, preferred_element_type=jnp.float32)  9.66 us
    dot_general x3, matrix products, per_device(): jnp.einsum('ngqk,knd->qngd', attention_probs, values_all[:key_end], prefe...  8.09 us
    convert_element_type x1, other arithmetic, per_device(): normed = (widened * lax.rsqrt(jnp.mean(widened * widened, axis=-1, keepdi...  7.88 us
    reduce_sum x1, other arithmetic, per_device(): jnp.mean(widened * widened, axis=-1, keepdims=True) + 1e-05  7.07 us
    dot_general x1, matrix products, per_device(): token_sums = jnp.dot(member, tokens, preferred_element_type=jnp.float32)  6.55 us
    dot_general x3, matrix products, per_device(): jnp.einsum('qngd,knd->ngqk', block_queries, keys_rot[:key_end], preferred...  5.99 us
  transfers between devices with their start and end apart: 2, of which 2 were waited for; matrix products, arithmetic and copies ran while one was open for 0% of the time, Pallas kernels for 0%

commit v1 on v0

--- a/solution.py
+++ b/solution.py
@@ -150,7 +150,7 @@
     mp_size = lax.axis_size("mp")
     mp_rank = lax.axis_index("mp")
     share_cols = model_width // mp_size
-    pooled = (token_sums + lax.psum(head_part, "mp")) / token_counts
+    pooled = (token_sums + jnp.sum(lax.all_gather(head_part, "mp"), axis=0)) / token_counts
     embedded = pooled * lax.rsqrt(jnp.mean(pooled * pooled, axis=-1, keepdims=True) + 1e-06)
     seq_total = episode_ids.shape[0]
     episodes = max(1, seq_total // (2 * WAYS))

time: 167 us -> 146 us (0.87)
  waiting for transfers between devices: 60.6 us -> 25.2 us
  blocking collectives: 0 us -> 17.4 us
  matrix products: 43.6 us -> 40.2 us
    psum x1 -> x0, waiting for transfers between devices: 37.5 us -> none  [per_device(): pooled = (token_sums + lax.psum(head_part, 'mp')) / token_counts]
    all_gather x0 -> x1, blocking collectives: none -> 17.4 us  [per_device(): lax.all_gather(head_part, 'mp')]
    dot_general x1, matrix products: 6.55 us -> 1.9 us  [per_device(): token_sums = jnp.dot(member, tokens, preferred_element_type=jnp.float32)]
    all_gather x1, waiting for transfers between devices: 23.1 us -> 25.2 us  [per_device(): lax.all_gather(embedded, 'dp', axis=0, tiled=True)]
    unnamed x22 -> x34, local copies, waits for them, and re-layouts: 5.64 us -> 5.68 us
  transfers between devices with their start and end apart: 2 -> 1, of which waited for: 2 -> 1; matrix products, arithmetic and copies ran while one was open for 0% -> 0% of each run, Pallas kernels for 0% -> 0%
where the time goes in v1:
time: 146 us; the launch traced here: 145 us
  matrix products  40.2 us (28%)
  other arithmetic  38.3 us (26%)
  waiting for transfers between devices  25.2 us (17%)
  blocking collectives  17.4 us (12%)
  between operations  14.5 us (10%)
  local copies, waits for them, and re-layouts  9.66 us (7%)
    all_gather x1, waiting for transfers between devices, per_device(): lax.all_gather(embedded, 'dp', axis=0, tiled=True)  25.2 us
    all_gather x1, blocking collectives, per_device(): lax.all_gather(head_part, 'mp')  17.4 us
    dot_general x1, matrix products, per_device(): jnp.dot(normed, w_query, preferred_element_type=jnp.float32)  9.66 us
    dot_general x3, matrix products, per_device(): jnp.einsum('ngqk,knd->qngd', attention_probs, values_all[:key_end], prefe...  8.83 us
    convert_element_type x1, other arithmetic, per_device(): normed = (widened * lax.rsqrt(jnp.mean(widened * widened, axis=-1, keepdi...  7.88 us
    reduce_sum x1, other arithmetic, per_device(): jnp.mean(widened * widened, axis=-1, keepdims=True) + 1e-05  7.07 us
    dot_general x3, matrix products, per_device(): jnp.einsum('qngd,knd->ngqk', block_queries, keys_rot[:key_end], preferred...  5.99 us
    unnamed x34, local copies, waits for them, and re-layouts  5.68 us
  transfers between devices with their start and end apart: 1, of which 1 were waited for; matrix products, arithmetic and copies ran while one was open for 0% of the time, Pallas kernels for 0%

profile of v1, /device:TPU:0, one launch (start us, length us, event | category | flops | bytes accessed | tf_op | source)
XLA Modules:
  0.0 145.2 jit_solution(11591893987354211136)
XLA Ops:
  8.9 7.1 %fusion = f32[1536]{0:T(1024)S(1)} fusion(bf16[1536,4096]{1,0:T(8,128)(2,1)} %param.11), kind=kLoop, calls=%fused_computation.2 | loop fusion | flops 18872832 | bytes 12589056 | tf_op jit(solution)/shard_map/reduce_sum | solution.py:92
  16.0 7.9 %fusion.2 = bf16[1536,4096]{1,0:T(8,128)(2,1)S(1)} fusion(bf16[1536,4096]{1,0:T(8,128)(2,1)} %param.11, f32[4096]{0:T(1024)S(1)} %convert_element_type.82, f32[1536]{0:T(1024)S(1)} %add_rsqrt_fusion), kind=kLoop, calls=%fused_computation.4 | loop fusion | flops 25165824 | bytes 25188352 | tf_op jit(solution)/shard_map/convert_element_type | solution.py:94
  23.9 3.4 %convolution_convert_fusion = bf16[1536,128]{1,0:T(8,128)(2,1)S(1)} fusion(bf16[1536,4096]{1,0:T(8,128)(2,1)S(1)} %fusion.2, bf16[4096,128]{1,0:T(8,128)(2,1)S(1)} %copy-done), kind=kOutput, calls=%fused_computation.35 | convolution fusion | flops 1610809344 | bytes 14024704 | tf_op jit(solution)/shard_map/dot_general | solution.py:109
  27.3 5.7 %convolution_bitcast_fusion = f32[1536,1,128]{0,2,1:T(8,128)S(1)} fusion(bf16[1536,4096]{1,0:T(8,128)(2,1)S(1)} %fusion.2, bf16[4096,128]{1,0:T(8,128)(2,1)} %param.14), kind=kOutput, calls=%fused_computation.34 | convolution fusion | flops 1610612736 | bytes 14417920 | tf_op jit(solution)/shard_map/dot_general | solution.py:103
  33.0 9.7 %fusion.87 = f32[1536,512]{0,1:T(8,128)} fusion(bf16[1536,4096]{1,0:T(8,128)(2,1)S(1)} %fusion.2, bf16[4096,512]{1,0:T(8,128)(2,1)} %param.13), kind=kOutput, calls=%fused_computation.143 | convolution fusion | flops 6442450944 | bytes 19922944 | tf_op jit(solution)/shard_map/dot_general | solution.py:96
  42.7 4.3 %multiply_cosine_fusion = (f32[1536,64]{1,0:T(8,128)}, f32[1536,64]{1,0:T(8,128)}) fusion(f32[64]{0:T(128)S(1)} %negate_power_fusion, f32[1536]{0:T(1024)S(1)} %convert_element_type.85), kind=kLoop, calls=%fused_computation.57 | loop fusion | flops 98304 | bytes 792832 | tf_op jit(solution)/shard_map/cos | solution.py:19
  47.0 1.6 %fusion.51 = (bf16[1536,1,64]{0,2,1:T(8,128)(2,1)S(1)}, bf16[1536,1,64]{0,2,1:T(8,128)(2,1)S(1)}) fusion(f32[1536,1,128]{0,2,1:T(8,128)S(1)} %convolution_bitcast_fusion, f32[64]{0:T(128)S(1)} %negate_power_fusion, f32[1536]{0:T(1024)S(1)} %convert_element_type.85), kind=kLoop, calls=%fused_computation.78 | loop fusion | flops 884736 | bytes 1186048 | tf_op jit(solution)/shard_map/convert.6
  48.6 3.3 %fusion.84 = (f32[1536,4,64]{0,2,1:T(8,128)}, f32[1536,4,64]{0,2,1:T(8,128)S(1)}) fusion(f32[1536,4,128]{0,2,1:T(8,128)} %bitcast.124), kind=kLoop, calls=%fused_computation.140 | loop fusion | bytes 6291456 | tf_op jit(solution)/shard_map/slice | solution.py:22
  51.9 3.3 %copy.51 = f32[1536,4,64]{2,0,1:T(8,128)} copy(f32[1536,4,64]{0,2,1:T(8,128)} %get-tuple-element.6) | data formatting | bytes 3145728
  55.2 2.3 %copy.50 = f32[1536,4,64]{2,0,1:T(8,128)} copy(f32[1536,4,64]{0,2,1:T(8,128)S(1)} %get-tuple-element.7) | data formatting | bytes 3145728
  58.5 4.0 %subtract_convert_fusion = (bf16[1536,4,64]{2,0,1:T(8,128)(2,1)S(1)}, bf16[1536,4,64]{2,0,1:T(8,128)(2,1)S(1)}) fusion(f32[1536,4,64]{2,0,1:T(8,128)} %copy.51, f32[1536,4,64]{2,0,1:T(8,128)} %copy.50, f32[1536,64]{1,0:T(8,128)} %get-tuple-element.11, f32[1536,64]{1,0:T(8,128)} %get-tuple-element.10), kind=kLoop, calls=%fused_computation.31 | loop fusion | flops 3145728 | bytes 5505024 | tf_op jit(solution)/shard_map/convert.4
  63.8 2.0 %fusion.6 = (f32[4,512]{1,0:T(4,128)S(1)}, f32[1024,512,4]{1,0,2:T(8,128)S(1)}) fusion(pred[512,1024]{0,1:T(8,128)(4,1)S(1)} %fusion.18, bf16[1536,4,64]{2,0,1:T(8,128)(2,1)S(1)} %get-tuple-element.4, bf16[1536,4,64]{2,0,1:T(8,128)(2,1)S(1)} %get-tuple-element.5, bf16[1536,1,64]{0,2,1:T(8,128)(2,1)S(1)} %get-tuple-element.9, ...), kind=kOutput, calls=%fused_computation.14 | convolution fusion | flops 544733184 | bytes 10887168 | tf_op jit(solution)/shard_map/qngd,knd->ngqk/dot_general | solution.py:122
  66.7 1.5 %fusion.30 = bf16[128,4,512]{2,0,1:T(8,128)(2,1)S(1)} fusion(f32[4,512]{1,0:T(4,128)S(1)} %fusion.12, f32[4,512]{1,0:T(4,128)S(1)} %get-tuple-element.24, f32[512,512,4]{1,0,2:T(8,128)S(1)} %get-tuple-element.25, pred[512,512]{0,1:T(8,128)(4,1)S(1)} %fusion.36, bf16[1536,128]{1,0:T(8,128)(2,1)S(1)} %convolution_convert_fusion), kind=kOutput, calls=%fused_computation.54 | convolution fusion | flops 273940480 | bytes 5128192 | tf_op jit(solution)/shard_map/ngqk,knd->qngd/dot_general | solution.py:131
  68.2 1.9 %fusion.5 = f32[4,512]{1,0:T(4,128)S(1)} fusion(f32[1024,512,4]{1,0,2:T(8,128)S(1)} %get-tuple-element.23, f32[4,512]{1,0:T(4,128)S(1)} %get-tuple-element.22, pred[512,1024]{0,1:T(8,128)(4,1)S(1)} %fusion.18), kind=kLoop, calls=%fused_computation.13 | loop fusion | flops 8386560 | bytes 8929280 | tf_op jit(solution)/shard_map/reduce_sum | solution.py:56
  70.1 2.7 %fusion.27 = bf16[128,4,512]{2,0,1:T(8,128)(2,1)S(1)} fusion(f32[4,512]{1,0:T(4,128)S(1)} %fusion.5, f32[4,512]{1,0:T(4,128)S(1)} %get-tuple-element.22, f32[1024,512,4]{1,0,2:T(8,128)S(1)} %get-tuple-element.23, pred[512,1024]{0,1:T(8,128)(4,1)S(1)} %fusion.18, bf16[1536,128]{1,0:T(8,128)(2,1)S(1)} %copy-done.11), kind=kOutput, calls=%fused_computation.53 | convolution fusion | flops 547618816 | bytes 9715712 | tf_op jit(solution)/shard_map/ngqk,knd->qngd/dot_general | solution.py:131
  72.8 1.7 %fusion.14 = pred[512,1536]{0,1:T(8,128)(4,1)S(1)} fusion(s32[512]{0:T(512)S(1)} %get-tuple-element.16, s32[512]{0:T(512)S(1)} %iota_add_fusion, s32[1536]{0:T(1024)S(1)} %copy-done.4, pred[512]{0:T(512)(128)(4,1)S(1)} %get-tuple-element.14), kind=kLoop, calls=%fused_computation.32 | loop fusion | flops 4718592 | bytes 797184 | tf_op jit(solution)/shard_map/or | solution.py:49
  74.6 2.8 %fusion.4 = (f32[4,512]{1,0:T(4,128)S(1)}, f32[1536,512,4]{1,0,2:T(8,128)S(1)}) fusion(pred[512,1536]{0,1:T(8,128)(4,1)S(1)} %fusion.14, bf16[1536,4,64]{2,0,1:T(8,128)(2,1)S(1)} %get-tuple-element.5, bf16[1536,4,64]{2,0,1:T(8,128)(2,1)S(1)} %get-tuple-element.4, bf16[1536,64]{0,1:T(8,128)(2,1)S(1)} %bitcast.123, bf16[1536,64]{0,1:T(8,128)(2,1)S(1)} %bitcast.122), kind=kOutput, calls=%fused_computation.9 | convolution fusion | flops 816576512 | bytes 15343616 | tf_op jit(solution)/shard_map/qngd,knd->ngqk/dot_general | solution.py:122
  77.4 2.8 %fusion.3 = f32[4,512]{1,0:T(4,128)S(1)} fusion(f32[1536,512,4]{1,0,2:T(8,128)S(1)} %get-tuple-element.21, f32[4,512]{1,0:T(4,128)S(1)} %get-tuple-element.20, pred[512,1536]{0,1:T(8,128)(4,1)S(1)} %fusion.14), kind=kLoop, calls=%fused_computation.8 | loop fusion | flops 12580864 | bytes 13385728 | tf_op jit(solution)/shard_map/reduce_sum | solution.py:56
  80.3 4.7 %fusion.33 = bf16[128,4,512]{2,0,1:T(8,128)(2,1)} fusion(f32[4,512]{1,0:T(4,128)S(1)} %fusion.3, f32[4,512]{1,0:T(4,128)S(1)} %get-tuple-element.20, f32[1536,512,4]{1,0,2:T(8,128)S(1)} %get-tuple-element.21, pred[512,1536]{0,1:T(8,128)(4,1)S(1)} %fusion.14, bf16[1536,128]{1,0:T(8,128)(2,1)S(1)} %copy-done.12), kind=kOutput, calls=%fused_computation.55 | convolution fusion | flops 821297152 | bytes 14303232 | tf_op jit(solution)/shard_map/ngqk,knd->qngd/dot_general | solution.py:131
  84.9 1.5 %fusion.21 = f32[8,512]{1,0:T(8,128)S(1)} fusion(bf16[512,512]{0,1:T(8,128)(2,1)} %bitcast.127, bf16[512,512]{0,1:T(8,128)(2,1)S(1)} %bitcast.126, bf16[512,512]{0,1:T(8,128)(2,1)S(1)} %bitcast.125, s32[8]{0:T(128)S(1)} %get-tuple-element.19, s32[8]{0:T(128)S(1)} %copy-done.5), kind=kOutput, calls=%fused_computation.43 | convolution fusion | flops 17338368 | bytes 1589312 | tf_op jit(solution)/shard_map/dot_general | solution.py:142
  87.8 17.4 %all-gather = f32[32,4096]{1,0:T(8,128)S(1)} all-gather(f32[8,4096]{1,0:T(8,128)S(1)} %convolution_add_fusion), channel_id=2, replica_groups=mesh['dp'=8,'mp'=4] {'mp'}, dimensions={0}, use_global_device_ids=true | all-gather | bytes 655360 | tf_op jit(solution)/shard_map/all_gather | solution.py:153
  105.3 1.9 %multiply_reduce_fusion.2 = (f32[8]{0:T(128)S(1)}, f32[8,4096]{1,0:T(8,128)S(1)}) fusion(f32[8]{0:T(128)S(1)} %get-tuple-element.18, f32[8,4096]{1,0:T(8,128)S(1)} %bitcast_reduce_fusion, bf16[1536,4096]{1,0:T(8,128)(2,1)S(1)} %bitcast.121, s32[8]{0:T(128)S(1)} %get-tuple-element.19, s32[8]{0:T(128)S(1)} %copy-done.5), kind=kOutput, calls=%fused_computation.94 | convolution fusion | flops 100831224 | bytes 12845184 | tf_op jit(solution)/shard_map/dot_general | solution.py:143
  108.1 25.2 %all-gather.3.cloned.1.call-done = f32[64,4096]{1,0:T(8,128)} async-done(((f32[8,4096]{1,0:T(8,128)}), f32[64,4096]{1,0:T(8,128)}) %all-gather.3.cloned.1.call-update) | async-done | bytes 1048592 | tf_op jit(solution)/shard_map/all_gather | solution.py:166
  133.3 1.8 %multiply_reduce_fusion.1 = (f32[32]{0:T(128)S(1)}, f32[32,4096]{1,0:T(8,128)S(1)}) fusion(f32[64,4096]{1,0:T(8,128)} %all-gather.3.cloned.1.call-done, s32[64]{0:T(128)S(1)} %multiply_add_fusion, pred[64]{0:T(512)(128)(4,1)S(1)} %broadcast_compare_fusion.3), kind=kOutput, calls=%fused_computation.76 | convolution fusion | flops 100929504 | bytes 1573312 | tf_op jit(solution)/shard_map/dot_general | solution.py:165
  (68 shorter events, 10.4 us)
Async XLA Ops:
  7.2 16.7 %copy-start = (bf16[4096,128]{1,0:T(8,128)(2,1)S(1)}, bf16[4096,128]{1,0:T(8,128)(2,1)}, u32[]{:S(2)}) copy-start(bf16[4096,128]{1,0:T(8,128)(2,1)} %param.15) | copy-start | bytes 3145732
  7.2 126.1 %all-gather.3.cloned.1.call-start = ((), (), s32[]{:S(2)}) async-start(), calls=%async_computation | async-start | bytes 1179648 | tf_op jit(solution)/shard_map/all_gather | solution.py:166
  8.8 7.1 %copy-start.3 = (s32[1536]{0:T(1024)}, s32[1536]{0:T(1024)S(1)}, u32[]{:S(2)}) copy-start(s32[1536]{0:T(1024)S(1)} %broadcast_add_fusion) | copy-start | bytes 18436
  8.8 7.1 %copy-start.6 = (bf16[4096]{0:T(1024)(128)(2,1)S(1)}, bf16[4096]{0:T(1024)(128)(2,1)}, u32[]{:S(2)}) copy-start(bf16[4096]{0:T(1024)(128)(2,1)} %param.12) | copy-start | bytes 24580
  27.3 39.4 %copy-start.10 = (bf16[1536,128]{1,0:T(8,128)(2,1)}, bf16[1536,128]{1,0:T(8,128)(2,1)S(1)}, u32[]{:S(2)}) copy-start(bf16[1536,128]{1,0:T(8,128)(2,1)S(1)} %convolution_convert_fusion) | copy-start | bytes 1179652
  51.9 5.9 %slice-start.3 = ((s32[1536]{0:T(1024)}), s32[1024]{0:T(1024)S(1)}, s32[]{:S(2)}) async-start(s32[1536]{0:T(1024)} %copy-done.3), calls=%async_computation.4 | async-start | bytes 8192 | tf_op jit(solution)/shard_map/slice | solution.py:43
  68.2 1.9 %copy-start.11 = (bf16[1536,128]{1,0:T(8,128)(2,1)S(1)}, bf16[1536,128]{1,0:T(8,128)(2,1)}, u32[]{:S(2)}) copy-start(bf16[1536,128]{1,0:T(8,128)(2,1)} %copy-done.10) | copy-start | bytes 1179652
  70.1 2.7 %copy-start.4 = (s32[1536]{0:T(1024)S(1)}, s32[1536]{0:T(1024)}, u32[]{:S(2)}) copy-start(s32[1536]{0:T(1024)} %copy-done.3) | copy-start | bytes 18436
  77.4 2.8 %copy-start.12 = (bf16[1536,128]{1,0:T(8,128)(2,1)S(1)}, bf16[1536,128]{1,0:T(8,128)(2,1)}, u32[]{:S(2)}) copy-start(bf16[1536,128]{1,0:T(8,128)(2,1)} %copy-done.10) | copy-start | bytes 1179652
  77.4 27.8 %slice-start = ((s8[12582912]{0:T(1024)(128)(4,1)}), s8[4194304]{0:T(1024)(128)(4,1)S(1)}, s32[]{:S(2)}) async-start(s8[12582912]{0:T(1024)(128)(4,1)} %bitcast.120), calls=%async_computation.1 | async-start | bytes 8388608
  80.2 4.7 %copy-start.5 = (s32[8]{0:T(128)S(1)}, s32[8]{0:T(128)}, u32[]{:S(2)}) copy-start(s32[8]{0:T(128)} %param.17) | copy-start | bytes 100
  80.2 6.2 %copy-start.2 = (bf16[512,4096]{1,0:T(8,128)(2,1)S(1)}, bf16[512,4096]{1,0:T(8,128)(2,1)}, u32[]{:S(2)}) copy-start(bf16[512,4096]{1,0:T(8,128)(2,1)} %param.16) | copy-start | bytes 12582916
  80.2 25.0 %slice-start.1 = ((s8[12582912]{0:T(1024)(128)(4,1)}), s8[4194304]{0:T(1024)(128)(4,1)S(1)}, s32[]{:S(2)}) async-start(s8[12582912]{0:T(1024)(128)(4,1)} %bitcast.120), calls=%async_computation.2 | async-start | bytes 8388608
  80.2 25.0 %slice-start.2 = ((s8[12582912]{0:T(1024)(128)(4,1)}), s8[4194304]{0:T(1024)(128)(4,1)S(1)}, s32[]{:S(2)}) async-start(s8[12582912]{0:T(1024)(128)(4,1)} %bitcast.120), calls=%async_computation.3 | async-start | bytes 8388608
  105.2 2.7 %copy-start.7 = (s32[64]{0:T(128)S(1)}, s32[64]{0:T(128)}, u32[]{:S(2)}) copy-start(s32[64]{0:T(128)} %param.21) | copy-start | bytes 772
  105.3 2.7 %copy-start.8 = (s32[64]{0:T(128)S(1)}, s32[64]{0:T(128)}, u32[]{:S(2)}) copy-start(s32[64]{0:T(128)} %param.19) | copy-start | bytes 772
  105.3 2.8 %copy-start.9 = (s32[64]{0:T(128)S(1)}, s32[64]{0:T(128)}, u32[]{:S(2)}) copy-start(s32[64]{0:T(128)} %param.20) | copy-start | bytes 772
  105.3 33.1 %copy-start.1 = (bf16[4096,128]{1,0:T(8,128)(2,1)S(1)}, bf16[4096,128]{1,0:T(8,128)(2,1)}, u32[]{:S(2)}) copy-start(bf16[4096,128]{1,0:T(8,128)(2,1)} %param.15) | copy-start | bytes 3145732
Sparse Core Ops, SparseCore 0:
  108.1 25.1 all-gather.2
